TPU v7x, 32 devices: a whole 2x2x4 slice. The times are simulated.
32 devices in a mesh: tm: 4 (over y, x), space: 8 (over z, core).
Axes of the slice: x: 2, y: 2, z: 4, core: 2. Of those that a mesh axis runs over, the one named last changes fastest.
Arguments:
- thermal_field: float32 [128, 49152], P(('tm', 'space')), may hold values from 245 to 255
- seasonal_bucket: int32 [128], replicated, may hold values from 0 to 45, as said below
- season_of_record: int32 [128], replicated, may hold values from 0 to 7
Outputs:
- anomaly: float32 [128, 49152], P(('tm', 'space'))
Inputs may be any that keep to these rules, and one draw needn't show every extreme that they name: `seasonal_bucket`: every group holds at least one day whose year is below 6.
All inputs are finite; a program needn't handle non-finite values.
Results may differ from a plain program's by a relative error of at most 0.0003.
Values sent between devices are 32-bit elements; how exact they have to be, the bound alone decides.
A program may use at most 64 MiB of HBM per device.

v0:
```python
import jax
import jax.numpy as jnp
from jax import lax
from jax.sharding import PartitionSpec as P

GROUPS = 46
BASE_YEARS = 6


def shards(thermal_field, seasonal_bucket, season_of_record):
    group_ids = jnp.arange(GROUPS, dtype=jnp.int32)
    member = (seasonal_bucket[None, :] == group_ids[:, None]).astype(jnp.float32)
    reference_seasons = member * (season_of_record < BASE_YEARS).astype(jnp.float32)[None, :]
    counts = jnp.sum(reference_seasons, axis=1)
    column_blocks = lax.all_to_all(
        thermal_field, ("tm", "space"), split_axis=1, concat_axis=0, tiled=True
    )
    bucket_aggregates = jnp.dot(
        reference_seasons,
        column_blocks,
        precision=lax.Precision.HIGHEST,
        preferred_element_type=jnp.float32,
    )
    climate = bucket_aggregates / counts[:, None]
    chosen_records = jnp.dot(
        member.T, climate, precision=lax.Precision.HIGHEST, preferred_element_type=jnp.float32
    )
    result = lax.all_to_all(
        column_blocks - chosen_records, ("tm", "space"), split_axis=0, concat_axis=1, tiled=True
    )
    return result


def solution(mesh):
    placed = (P(("tm", "space"), None), P(), P())
    return jax.shard_map(
        shards, mesh=mesh, in_specs=placed, out_specs=P(("tm", "space"), None), check_vma=False
    )
```

profile of v0, /device:TPU:0, one launch (start us, length us, event | category | flops | bytes accessed | tf_op | source)
XLA Modules:
  0.0 55.6 jit_solution(11356422681699996724)
XLA Ops:
  0.0 0.0 copy-start.1
  0.0 7.3 %all-to-all-start = ((f32[4,32,1536]{2,0,1:T(4,128)}), f32[4,32,1536]{2,0,1:T(4,128)S(1)}, u32[]{:S(2)}, u32[]{:S(2)}) async-start(f32[4,32,1536]{2,0,1:T(4,128)} %bitcast.9), calls=%async_computation | async-start | bytes 1572864 | tf_op jit(solution)/shard_map/all_to_all | solution.py:15
  7.3 0.0 copy-done.1
  7.3 0.0 copy-start
  7.4 0.6 %copy-done = s32[128]{0:T(128)S(1)} copy-done((s32[128]{0:T(128)S(1)}, s32[128]{0:T(128)}, u32[]{:S(2)}) %copy-start) | copy-done | bytes 536
  8.0 0.1 select_reduce_fusion
  8.1 21.1 %all-to-all-done = f32[4,32,1536]{2,0,1:T(4,128)S(1)} async-done(((f32[4,32,1536]{2,0,1:T(4,128)}), f32[4,32,1536]{2,0,1:T(4,128)S(1)}, u32[]{:S(2)}, u32[]{:S(2)}) %all-to-all-start) | async-done | bytes 786464 | tf_op jit(solution)/shard_map/all_to_all | solution.py:15
  29.2 0.3 all_to_all.31
  29.5 0.5 convolution_divide_fusion
  30.0 0.5 convolution_subtract_fusion
  30.5 0.2 all_to_all.32
  30.8 24.0 %all_to_all.38 = f32[32,4,1536]{2,1,0:T(4,128)S(1)} all-to-all(f32[32,4,1536]{2,1,0:T(4,128)S(1)} %all_to_all.32), channel_id=1, replica_groups=mesh['tm'=4,'space'=8] {'tm','space'}, dimensions={0} | all-to-all | bytes 1572864 | tf_op jit(solution)/shard_map/all_to_all | solution.py:28
  54.7 0.9 %copy.9 = f32[4,49152]{1,0:T(4,128)} copy(f32[4,49152]{1,0:T(4,128)S(1)} %bitcast.8) | data formatting | bytes 1572864
  (1 shorter events, 0.0 us)
Async XLA Ops:
  0.0 7.3 %copy-start.1 = (s32[128]{0:T(128)S(1)}, s32[128]{0:T(128)}, u32[]{:S(2)}) copy-start(s32[128]{0:T(128)} %param.5) | copy-start | bytes 1540
  0.0 29.2 %all-to-all-start = ((f32[4,32,1536]{2,0,1:T(4,128)}), f32[4,32,1536]{2,0,1:T(4,128)S(1)}, u32[]{:S(2)}, u32[]{:S(2)}) async-start(f32[4,32,1536]{2,0,1:T(4,128)} %bitcast.9), calls=%async_computation | async-start | bytes 1572864 | tf_op jit(solution)/shard_map/all_to_all | solution.py:15
  7.3 0.7 %copy-start = (s32[128]{0:T(128)S(1)}, s32[128]{0:T(128)}, u32[]{:S(2)}) copy-start(s32[128]{0:T(128)} %param.4) | copy-start | bytes 1540
where the time goes:
time: 55.8 us; the launch traced here: 55.6 us
  blocking collectives  24 us (43%)
  waiting for transfers between devices  21.1 us (38%)
  starting transfers between devices  7.33 us (13%)
  local copies, waits for them, and re-layouts  2.02 us (4%)
  matrix products  1.05 us (2%)
    all_to_all x1, blocking collectives, shards(): lax.all_to_all(column_blocks - chosen_records, ('tm', 'space'), split_axi...  24 us
    all_to_all x1, waiting for transfers between devices, shards(): lax.all_to_all(thermal_field, ('tm', 'space'), split_axis=1, concat_axis=...  21.1 us
    all_to_all x1, starting transfers between devices, shards(): lax.all_to_all(thermal_field, ('tm', 'space'), split_axis=1, concat_axis=...  7.33 us
    unnamed x5, local copies, waits for them, and re-layouts  1.52 us
  transfers between devices with their start and end apart: 1, of which 1 were waited for; matrix products, arithmetic and copies ran while one was open for 0% of the time, Pallas kernels for 0%

commit v1 on v0

v1 whole, which is shorter than its diff:
```python
import functools

import jax
import jax.numpy as jnp
from jax import lax
from jax.experimental import pallas as pl
from jax.experimental.pallas import tpu as pltpu
from jax.sharding import PartitionSpec as P

BASE_YEARS = 6
CHUNKS = 3


def for_peers(nt, ns, body):
    t, s = lax.axis_index("tm"), lax.axis_index("space")

    def one(dt, ds):
        pt, ps = lax.rem(t + dt, nt), lax.rem(s + ds, ns)
        body(pt, ps, pt * ns + ps)

    def step(i, carry):
        one(lax.rem(i, nt), 1 + lax.rem(i // nt + (ns // 2 - 1), ns - 1))
        return carry

    lax.fori_loop(0, nt * (ns - 1), step, 0)
    for dt in range(1, nt):
        one(dt, 0)


def kernel(nt, ns, chunks, x_hbm, bucket_ref, season_ref, out_ref,
           xv, recv, y, load_sem, own_sem, send1, recv1, send2, recv2):
    n = nt * ns
    rows, cells = x_hbm.shape
    mine = cells // n
    c = mine // chunks
    days = rows * n
    me = lax.axis_index("tm") * ns + lax.axis_index("space")

    load = pltpu.make_async_copy(x_hbm, xv, load_sem)
    load.start()
    own = []
    for k in range(chunks):
        own.append(pltpu.make_async_copy(
            x_hbm.at[:, pl.ds(pl.multiple_of(me * mine + k * c, 128), c)],
            recv.at[k, me], own_sem.at[k]))
        own[k].start()

    barrier = pltpu.get_barrier_semaphore()
    for_peers(nt, ns, lambda pt, ps, p: pl.semaphore_signal(
        barrier, inc=1, device_id=(pt, ps), device_id_type=pl.DeviceIdType.MESH))
    pl.semaphore_wait(barrier, n - 1)
    load.wait()

    for k in range(chunks):
        def push(pt, ps, p, k=k):
            pltpu.make_async_remote_copy(
                src_ref=xv.at[:, pl.ds(pl.multiple_of(p * mine + k * c, 128), c)],
                dst_ref=recv.at[k, me],
                send_sem=send1.at[k], recv_sem=recv1.at[k],
                device_id=(pt, ps), device_id_type=pl.DeviceIdType.MESH).start()
        for_peers(nt, ns, push)

    bucket = jnp.broadcast_to(bucket_ref[...], (days, days))
    season = jnp.broadcast_to(season_ref[...], (days, days))
    member = jnp.where((bucket == bucket.T) & (season < BASE_YEARS), 1.0, 0.0)
    inverse = 1.0 / jnp.sum(member, axis=1, keepdims=True)
    member = member.astype(jnp.bfloat16)

    def all_of(ref, sem):
        part = ref.at[pl.ds(0, n - 1)]
        pltpu.make_async_copy(part, part, sem).wait()

    for k in range(chunks):
        own[k].wait()
        all_of(recv.at[k], recv1.at[k])
        x = recv[k].reshape(days, c)
        high = x.astype(jnp.bfloat16)
        rest = x - high.astype(jnp.float32)
        middle = rest.astype(jnp.bfloat16)
        low = (rest - middle.astype(jnp.float32)).astype(jnp.bfloat16)
        total = jnp.dot(member, low, preferred_element_type=jnp.float32)
        total += jnp.dot(member, middle, preferred_element_type=jnp.float32)
        total += jnp.dot(member, high, preferred_element_type=jnp.float32)
        y[k] = (x - total * inverse).reshape(n, rows, c)

        def back(pt, ps, p, k=k):
            pltpu.make_async_remote_copy(
                src_ref=y.at[k, p],
                dst_ref=out_ref.at[:, pl.ds(pl.multiple_of(me * mine + k * c, 128), c)],
                send_sem=send2.at[k], recv_sem=recv2.at[k],
                device_id=(pt, ps), device_id_type=pl.DeviceIdType.MESH).start()
        for_peers(nt, ns, back)
        out_ref[:, pl.ds(pl.multiple_of(me * mine + k * c, 128), c)] = y[k, me]

    for k in range(chunks):
        all_of(recv.at[k], send1.at[k])
        all_of(recv.at[k], recv2.at[k])
        all_of(recv.at[k], send2.at[k])


def solution(mesh):
    nt, ns = mesh.shape["tm"], mesh.shape["space"]
    n = nt * ns

    def shards(thermal_field, seasonal_bucket, season_of_record):
        rows, cells = thermal_field.shape
        c = cells // n // CHUNKS
        vmem = pl.BlockSpec(memory_space=pltpu.VMEM)
        sems = pltpu.SemaphoreType.DMA
        return pl.pallas_call(
            functools.partial(kernel, nt, ns, CHUNKS),
            out_shape=jax.ShapeDtypeStruct((rows, cells), jnp.float32),
            in_specs=[pl.BlockSpec(memory_space=pl.ANY), vmem, vmem],
            out_specs=vmem,
            scratch_shapes=[
                pltpu.VMEM((rows, cells), jnp.float32),
                pltpu.VMEM((CHUNKS, n, rows, c), jnp.float32),
                pltpu.VMEM((CHUNKS, n, rows, c), jnp.float32),
                sems, sems((CHUNKS,)), sems((CHUNKS,)), sems((CHUNKS,)),
                sems((CHUNKS,)), sems((CHUNKS,)),
            ],
            compiler_params=pltpu.CompilerParams(collective_id=0, has_side_effects=True),
            name="anomaly",
        )(thermal_field, seasonal_bucket.reshape(1, -1), season_of_record.reshape(1, -1))

    placed = (P(("tm", "space"), None), P(), P())
    return jax.shard_map(
        shards, mesh=mesh, in_specs=placed, out_specs=P(("tm", "space"), None), check_vma=False
    )
```

time: 55.8 us -> 45.9 us (0.82)
  Pallas kernels: 0 us -> 43.6 us
  blocking collectives: 24 us -> 0 us
  waiting for transfers between devices: 21.1 us -> 0 us
  starting transfers between devices: 7.33 us -> 0 us
  matrix products: 1.05 us -> 0 us
    pallas_call x0 -> x1, Pallas kernels: none -> 43.6 us  [shards(): pl.pallas_call(functools.partial(kernel, nt, ns, CHUNKS), out_shape=jax.S...]
    all_to_all x1 -> x0, blocking collectives: 24 us -> none  [shards(): lax.all_to_all(column_blocks - chosen_records, ('tm', 'space'), split_axi...]
    all_to_all x1 -> x0, waiting for transfers between devices: 21.1 us -> none  [shards(): lax.all_to_all(thermal_field, ('tm', 'space'), split_axis=1, concat_axis=...]
    all_to_all x1 -> x0, starting transfers between devices: 7.33 us -> none  [shards(): lax.all_to_all(thermal_field, ('tm', 'space'), split_axis=1, concat_axis=...]
    dot_general x2 -> x0, matrix products: 1.05 us -> none  [the longest x1 0.54 us: shards(): jnp.dot(reference_seasons, column_blocks, precision=lax.Precision.HIGHEST...]
    unnamed x5 -> x1, local copies, waits for them, and re-layouts: 1.52 us -> 2.06 us
  transfers between devices with their start and end apart: 1 -> 0, of which waited for: 1 -> 0; matrix products, arithmetic and copies ran while one was open for 0% -> 0% of each run, Pallas kernels for 0% -> 0%
where the time goes in v1:
time: 45.9 us; the launch traced here: 45.7 us
  Pallas kernels  43.6 us (95%)
  local copies, waits for them, and re-layouts  2.06 us (4%)
    pallas_call x1, Pallas kernels, shards(): pl.pallas_call(functools.partial(kernel, nt, ns, CHUNKS), out_shape=jax.S...  43.6 us
    unnamed x1, local copies, waits for them, and re-layouts  2.06 us

profile of v1, /device:TPU:0, one launch (start us, length us, event | category | flops | bytes accessed | tf_op | source)
XLA Modules:
  0.0 45.7 jit_solution(16709208448948962575)
XLA Ops:
  0.0 43.6 %anomaly.1 = f32[4,49152]{1,0:T(4,128)} custom-call(f32[4,49152]{1,0:T(4,128)} %x_hbm.1, s32[1,128]{1,0:T(1,128)} %bitcast.2, s32[1,128]{1,0:T(1,128)} %bitcast.3), custom_call_target="tpu_custom_call" | custom-call | tf_op jit(solution)/shard_map/anomaly/pallas_call | solution.py:110
  43.6 2.1 %copy.5 = f32[4,49152]{1,0:T(4,128)} copy(f32[4,49152]{1,0:T(4,128)} %anomaly.1) | data formatting | bytes 1572864

commit v2 on v1

--- a/solution.py
+++ b/solution.py
@@ -27,8 +27,8 @@
         one(dt, 0)
 
 
-def kernel(nt, ns, chunks, x_hbm, bucket_ref, season_ref, out_ref,
-           xv, recv, y, load_sem, own_sem, send1, recv1, send2, recv2):
+def kernel(nt, ns, chunks, x_hbm, bucket_hbm, season_hbm, out_ref,
+           calendar, date_sem, xv, recv, y, load_sem, own_sem, send1, recv1, send2, recv2):
     n = nt * ns
     rows, cells = x_hbm.shape
     mine = cells // n
@@ -38,6 +38,10 @@
 
     load = pltpu.make_async_copy(x_hbm, xv, load_sem)
     load.start()
+    dates = [pltpu.make_async_copy(ref, calendar.at[i], date_sem.at[i])
+             for i, ref in enumerate((bucket_hbm, season_hbm))]
+    for date in dates:
+        date.start()
     own = []
     for k in range(chunks):
         own.append(pltpu.make_async_copy(
@@ -60,8 +64,10 @@
                 device_id=(pt, ps), device_id_type=pl.DeviceIdType.MESH).start()
         for_peers(nt, ns, push)
 
-    bucket = jnp.broadcast_to(bucket_ref[...], (days, days))
-    season = jnp.broadcast_to(season_ref[...], (days, days))
+    for date in dates:
+        date.wait()
+    bucket = jnp.broadcast_to(calendar[0], (days, days))
+    season = jnp.broadcast_to(calendar[1], (days, days))
     member = jnp.where((bucket == bucket.T) & (season < BASE_YEARS), 1.0, 0.0)
     inverse = 1.0 / jnp.sum(member, axis=1, keepdims=True)
     member = member.astype(jnp.bfloat16)
@@ -104,24 +110,26 @@
 
     def shards(thermal_field, seasonal_bucket, season_of_record):
         rows, cells = thermal_field.shape
-        c = cells // n // CHUNKS
+        c, days = cells // n // CHUNKS, rows * n
         vmem = pl.BlockSpec(memory_space=pltpu.VMEM)
         sems = pltpu.SemaphoreType.DMA
         return pl.pallas_call(
             functools.partial(kernel, nt, ns, CHUNKS),
             out_shape=jax.ShapeDtypeStruct((rows, cells), jnp.float32),
-            in_specs=[pl.BlockSpec(memory_space=pl.ANY), vmem, vmem],
+            in_specs=[pl.BlockSpec(memory_space=pltpu.HBM)] * 3,
             out_specs=vmem,
             scratch_shapes=[
+                pltpu.VMEM((2, 1, days), jnp.int32), sems((2,)),
                 pltpu.VMEM((rows, cells), jnp.float32),
                 pltpu.VMEM((CHUNKS, n, rows, c), jnp.float32),
                 pltpu.VMEM((CHUNKS, n, rows, c), jnp.float32),
                 sems, sems((CHUNKS,)), sems((CHUNKS,)), sems((CHUNKS,)),
                 sems((CHUNKS,)), sems((CHUNKS,)),
             ],
-            compiler_params=pltpu.CompilerParams(collective_id=0, has_side_effects=True),
+            compiler_params=pltpu.CompilerParams(collective_id=0, has_side_effects=True, vmem_limit_bytes=24 * 2**20),
             name="anomaly",
-        )(thermal_field, seasonal_bucket.reshape(1, -1), season_of_record.reshape(1, -1))
+        )(*(pltpu.with_memory_space_constraint(a, pltpu.HBM) for a in (
+            thermal_field, seasonal_bucket.reshape(1, -1), season_of_record.reshape(1, -1))))
 
     placed = (P(("tm", "space"), None), P(), P())
     return jax.shard_map(

time: 45.9 us -> 43.4 us (0.946)
  Pallas kernels: 43.6 us -> 42.3 us
  local copies, waits for them, and re-layouts: 2.06 us -> 0.88 us
    pallas_call x1, Pallas kernels: 43.6 us -> 42.3 us  [shards(): pl.pallas_call(functools.partial(kernel, nt, ns, CHUNKS), out_shape=jax.S...]
    unnamed x1, local copies, waits for them, and re-layouts: 2.06 us -> 0.88 us
where the time goes in v2:
time: 43.4 us; the launch traced here: 43.2 us
  Pallas kernels  42.3 us (97%)
  local copies, waits for them, and re-layouts  0.88 us (2%)
    pallas_call x1, Pallas kernels, shards(): pl.pallas_call(functools.partial(kernel, nt, ns, CHUNKS), out_shape=jax.S...  42.3 us
    unnamed x1, local copies, waits for them, and re-layouts  0.88 us

profile of v2, /device:TPU:0, one launch (start us, length us, event | category | flops | bytes accessed | tf_op | source)
XLA Modules:
  0.0 43.2 jit_solution(5895439860418672176)
XLA Ops:
  0.0 42.3 %anomaly.1 = f32[4,49152]{1,0:T(4,128)S(1)} custom-call(f32[4,49152]{1,0:T(4,128)} %x_hbm.1, s32[1,128]{1,0:T(1,128)} %bitcast.2, s32[1,128]{1,0:T(1,128)} %bitcast.3), custom_call_target="tpu_custom_call" | custom-call | tf_op jit(solution)/shard_map/anomaly/pallas_call | solution.py:116
  42.4 0.9 %copy.5 = f32[4,49152]{1,0:T(4,128)} copy(f32[4,49152]{1,0:T(4,128)S(1)} %anomaly.1) | data formatting | bytes 1572864

commit v3 on v0

v3 whole, which is shorter than its diff:
```python
import functools

import jax
import jax.numpy as jnp
from jax import lax
from jax.experimental import pallas as pl
from jax.experimental.pallas import tpu as pltpu
from jax.sharding import PartitionSpec as P

GROUPS = 46
BASE_YEARS = 6
CHUNKS = 8
LAG = 2
LEAD = 3
SHARE = 2
MESH = pl.DeviceIdType.MESH


def exact_dot(mask, x):
    high = x.astype(jnp.bfloat16)
    rest = x - high.astype(jnp.float32)
    middle = rest.astype(jnp.bfloat16)
    low = (rest - middle.astype(jnp.float32)).astype(jnp.bfloat16)
    total = jnp.dot(mask, low, preferred_element_type=jnp.float32)
    total += jnp.dot(mask, middle, preferred_element_type=jnp.float32)
    return total + jnp.dot(mask, high, preferred_element_type=jnp.float32)


def kernel(nt, ns, chunks, lag, lead, x_hbm, bucket_hbm, season_hbm, out_ref,
           calendar, date_sem, xv, recv, sums, other, y, load_sem,
           send1, recv1, send2, recv2, send3, recv3,
           got, done, send4, recv4, send5, recv5):
    nh, nq = ns // 2, ns // 4
    half, owners = nt * nh, nt * nq
    when = chunks - 1
    when_other = chunks // 2
    rows, cells = x_hbm.shape
    n = nt * ns
    direct = cells // SHARE // n
    start = direct * n
    mine = (cells - start) // owners
    c = mine // chunks
    days = rows * nt * ns
    t, s = lax.axis_index("tm"), lax.axis_index("space")
    h = s // nh
    local = s - h * nh
    first = nq * (1 - h)
    place = local - first
    is_owner = (place >= 0) & (place < nq)
    slot = t * nh + local
    partner = s + nq * (1 - 2 * h)

    load = pltpu.make_async_copy(x_hbm, xv, load_sem)
    load.start()
    dates = [pltpu.make_async_copy(ref, calendar.at[i], date_sem.at[i])
             for i, ref in enumerate((bucket_hbm, season_hbm))]
    for date in dates:
        date.start()

    def to_owners(body, others):
        for dq in range(nq):
            for dt in range(nt):
                if others and dt == dq == 0:
                    continue
                pt, pq = lax.rem(t + dt, nt), lax.rem(place + nq + dq, nq)
                body(pt, h * nh + first + pq, pt * nq + pq)

    def to_half(body):
        for dl in [(nh // 2 + i) % nh for i in range(nh)]:
            for dt in range(nt):
                if dt == dl == 0:
                    continue
                pt, at = lax.rem(t + dt, nt), lax.rem(local + dl, nh)
                body(pt, h * nh + at, pt * nh + at)

    barrier = pltpu.get_barrier_semaphore()

    def greet(pt, ps, p):
        pl.semaphore_signal(barrier, inc=1, device_id=(pt, ps), device_id_type=MESH)

    def to_all(body):
        for ds in [(nh + i) % ns for i in range(ns)]:
            for dt in range(nt):
                if dt == ds == 0:
                    continue
                pt, ps = lax.rem(t + dt, nt), lax.rem(s + ds, ns)
                body(pt, ps, pt * ns + ps)

    to_all(greet)
    pl.semaphore_wait(barrier, n - 1)
    who = t * ns + s
    own = pl.ds(pl.multiple_of(who * direct, 128), direct)

    def push(k, others):
        def one(pt, ps, p):
            pltpu.make_async_remote_copy(
                src_ref=xv.at[:, pl.ds(pl.multiple_of(start + p * mine + k * c, 128), c)],
                dst_ref=recv.at[k, slot], send_sem=send1.at[k], recv_sem=recv1.at[k],
                device_id=(pt, ps), device_id_type=MESH).start()
        to_owners(one, others)

    load.wait()

    def push_direct(pt, ps, p):
        pltpu.make_async_remote_copy(
            src_ref=xv.at[:, pl.ds(pl.multiple_of(p * direct, 128), direct)],
            dst_ref=got.at[who], send_sem=send4, recv_sem=recv4,
            device_id=(pt, ps), device_id_type=MESH).start()
    to_all(push_direct)
    got[who] = xv[:, own]
    for date in dates:
        date.wait()

    def all_direct(sem):
        part = got.at[pl.ds(0, n - 1)]
        pltpu.make_async_copy(part, part, sem).wait()

    def finish_direct():
        bucket = jnp.broadcast_to(calendar[0], (days, days))
        season = jnp.broadcast_to(calendar[1], (days, days))
        same = jnp.where((bucket == bucket.T) & (season < BASE_YEARS), 1.0, 0.0)
        inverse = 1.0 / jnp.sum(same, axis=1, keepdims=True)
        all_direct(recv4)
        x = got[...].reshape(days, direct)
        mean = exact_dot(same.astype(jnp.bfloat16), x) * inverse
        done[...] = (x - mean).reshape(n, rows, direct)

        def back_direct(pt, ps, p):
            pltpu.make_async_remote_copy(
                src_ref=done.at[p], dst_ref=out_ref.at[:, own],
                send_sem=send5, recv_sem=recv5,
                device_id=(pt, ps), device_id_type=MESH).start()
        to_all(back_direct)
        out_ref[:, own] = done[who]

    def all_of(count, sem):
        part = recv.at[0, pl.ds(0, count)]
        pltpu.make_async_copy(part, part, sem).wait()

    @pl.when(is_owner)
    def _():
        for k in range(min(lead, chunks)):
            push(k, True)
        me = t * nq + place
        base = pl.multiple_of(start + me * mine, 128)
        padded = sums.shape[1]

        bucket, season = calendar[0], calendar[1]
        key = jnp.where(season < BASE_YEARS, bucket, -1)
        width = nh * rows
        here = half * rows
        order = lax.broadcasted_iota(jnp.int32, (here, days), 0)
        day = (order // width) * (2 * width) + h * width + lax.rem(order, width)
        pick = day == lax.broadcasted_iota(jnp.int32, (here, days), 1)

        def of_half(row):
            return jnp.sum(jnp.where(pick, row, 0), axis=1, keepdims=True)

        member = of_half(bucket) == lax.broadcasted_iota(jnp.int32, (here, padded), 1)
        member = jnp.where(member, 1.0, 0.0).astype(jnp.bfloat16)
        key_row = jnp.broadcast_to(of_half(key), (here, here)).T[:1]
        group = lax.broadcasted_iota(jnp.int32, (padded, here), 0)
        baseline = jnp.where(group == key_row, 1.0, 0.0).astype(jnp.bfloat16)
        counted = lax.broadcasted_iota(jnp.int32, (padded, days), 0) == key
        counts = jnp.sum(jnp.where(counted, 1.0, 0.0), axis=1, keepdims=True)
        inverse = 1.0 / jnp.maximum(counts, 1.0)

        def swap(k):
            return pltpu.make_async_remote_copy(
                src_ref=sums.at[k], dst_ref=other.at[k],
                send_sem=send2.at[k], recv_sem=recv2.at[k],
                device_id=(t, partner), device_id_type=MESH)

        def finish(k):
            swap(k).wait_recv()
            climate = (sums[k] + other[k]) * inverse
            x = recv[k].reshape(here, c)
            y[k] = (x - exact_dot(member, climate)).reshape(half, rows, c)
            at = pl.ds(pl.multiple_of(base + k * c, 128), c)

            def back(pt, ps, p):
                pltpu.make_async_remote_copy(
                    src_ref=y.at[k, p], dst_ref=out_ref.at[:, at],
                    send_sem=send3.at[k], recv_sem=recv3.at[k],
                    device_id=(pt, ps), device_id_type=MESH).start()
            to_half(back)
            out_ref[:, at] = y[k, slot]

        for k in range(chunks):
            if k + lead < chunks:
                push(k + lead, True)
            recv[k, slot] = xv[:, pl.ds(pl.multiple_of(base + k * c, 128), c)]
            all_of(half - 1, recv1.at[k])
            sums[k] = exact_dot(baseline, recv[k].reshape(here, c))
            swap(k).start()
            if k == when:
                finish_direct()
            if k >= lag:
                finish(k - lag)
        for k in range(max(chunks - lag, 0), chunks):
            finish(k)

        for k in range(chunks):
            all_of(owners - 1, send1.at[k])
            swap(k).wait_send()
            all_of(owners - 1, recv3.at[k])
            all_of(half - 1, send3.at[k])

    @pl.when(jnp.logical_not(is_owner))
    def _():
        for k in range(chunks):
            push(k, False)
        for k in range(chunks):
            all_of(owners, send1.at[k])
            if k == when_other:
                finish_direct()
            all_of(owners, recv3.at[k])

    all_direct(send4)
    all_direct(recv5)
    all_direct(send5)


def solution(mesh):
    nt, ns = mesh.shape["tm"], mesh.shape["space"]
    half, owners = nt * (ns // 2), nt * (ns // 4)

    def shards(thermal_field, seasonal_bucket, season_of_record):
        rows, cells = thermal_field.shape
        n = nt * ns
        direct = cells // SHARE // n
        c, days = (cells - direct * n) // owners // CHUNKS, rows * n
        sems = pltpu.SemaphoreType.DMA
        per_chunk = sems((CHUNKS,))
        vmem = functools.partial(pltpu.VMEM, dtype=jnp.float32)
        return pl.pallas_call(
            functools.partial(kernel, nt, ns, CHUNKS, LAG, LEAD),
            out_shape=jax.ShapeDtypeStruct((rows, cells), jnp.float32),
            in_specs=[pl.BlockSpec(memory_space=pltpu.HBM)] * 3,
            out_specs=pl.BlockSpec(memory_space=pltpu.VMEM),
            scratch_shapes=[
                pltpu.VMEM((2, 1, days), jnp.int32), sems((2,)),
                vmem((rows, cells)),
                vmem((CHUNKS, half, rows, c)),
                vmem((CHUNKS, GROUPS, c)),
                vmem((CHUNKS, GROUPS, c)),
                vmem((CHUNKS, half, rows, c)),
                sems, per_chunk, per_chunk, per_chunk, per_chunk,
                per_chunk, per_chunk,
                vmem((n, rows, direct)), vmem((n, rows, direct)),
                sems, sems, sems, sems,
            ],
            compiler_params=pltpu.CompilerParams(
                collective_id=0, has_side_effects=True, vmem_limit_bytes=36 * 2**20),
            name="anomaly",
        )(*(pltpu.with_memory_space_constraint(a, pltpu.HBM) for a in (
            thermal_field, seasonal_bucket.reshape(1, -1), season_of_record.reshape(1, -1))))

    placed = (P(("tm", "space"), None), P(), P())
    return jax.shard_map(
        shards, mesh=mesh, in_specs=placed, out_specs=P(("tm", "space"), None), check_vma=False
    )
```

time: 55.8 us -> 42.3 us (0.76)
  Pallas kernels: 0 us -> 41.2 us
  blocking collectives: 24 us -> 0 us
  waiting for transfers between devices: 21.1 us -> 0 us
  starting transfers between devices: 7.33 us -> 0 us
  local copies, waits for them, and re-layouts: 2.02 us -> 0.88 us
  matrix products: 1.05 us -> 0 us
    pallas_call x0 -> x1, Pallas kernels: none -> 41.2 us  [shards(): pl.pallas_call(functools.partial(kernel, nt, ns, CHUNKS, LAG, LEAD), out_...]
    all_to_all x1 -> x0, blocking collectives: 24 us -> none  [shards(): lax.all_to_all(column_blocks - chosen_records, ('tm', 'space'), split_axi...]
    all_to_all x1 -> x0, waiting for transfers between devices: 21.1 us -> none  [shards(): lax.all_to_all(thermal_field, ('tm', 'space'), split_axis=1, concat_axis=...]
    all_to_all x1 -> x0, starting transfers between devices: 7.33 us -> none  [shards(): lax.all_to_all(thermal_field, ('tm', 'space'), split_axis=1, concat_axis=...]
    dot_general x2 -> x0, matrix products: 1.05 us -> none  [the longest x1 0.54 us: shards(): jnp.dot(reference_seasons, column_blocks, precision=lax.Precision.HIGHEST...]
    unnamed x5 -> x1, local copies, waits for them, and re-layouts: 1.52 us -> 0.88 us
  transfers between devices with their start and end apart: 1 -> 0, of which waited for: 1 -> 0; matrix products, arithmetic and copies ran while one was open for 0% -> 0% of each run, Pallas kernels for 0% -> 0%
where the time goes in v3:
time: 42.3 us; the launch traced here: 42.1 us
  Pallas kernels  41.2 us (97%)
  local copies, waits for them, and re-layouts  0.88 us (2%)
    pallas_call x1, Pallas kernels, shards(): pl.pallas_call(functools.partial(kernel, nt, ns, CHUNKS, LAG, LEAD), out_...  41.2 us
    unnamed x1, local copies, waits for them, and re-layouts  0.88 us

profile of v3, /device:TPU:0, one launch (start us, length us, event | category | flops | bytes accessed | tf_op | source)
XLA Modules:
  0.0 42.1 jit_solution(16612529646077189146)
XLA Ops:
  0.0 41.2 %anomaly.1 = f32[4,49152]{1,0:T(4,128)S(1)} custom-call(f32[4,49152]{1,0:T(4,128)} %x_hbm.1, s32[1,128]{1,0:T(1,128)} %bitcast.2, s32[1,128]{1,0:T(1,128)} %bitcast.3), custom_call_target="tpu_custom_call" | custom-call | tf_op jit(solution)/shard_map/anomaly/pallas_call | solution.py:236
  41.3 0.9 %copy.5 = f32[4,49152]{1,0:T(4,128)} copy(f32[4,49152]{1,0:T(4,128)S(1)} %anomaly.1) | data formatting | bytes 1572864
